TPU v7x, 32 devices: a whole 2x2x4 slice. The times are simulated.
32 devices in a mesh: groups: 2 (over y), expert: 4 (over z), hidden: 4 (over x, core).
Axes of the slice: x: 2, y: 2, z: 4, core: 2. Of those that a mesh axis runs over, the one named last changes fastest.
Arguments:
- tokens: bfloat16 [512, 4096], P(('groups', 'expert'), 'hidden'), parts along dimension 0, may hold values from -6 to 6
- norm_gain: bfloat16 [4096], P('hidden'), may hold values from 0.25 to 1.75
- gate_proj: bfloat16 [64, 768, 4096], P('expert', 'hidden'), may hold values from -0.09375 to 0.09375
- up_proj: bfloat16 [64, 768, 4096], P('expert', 'hidden'), may hold values from -0.09375 to 0.09375
- down_proj: bfloat16 [64, 768, 4096], P('expert', 'hidden'), may hold values from -0.21875 to 0.21875
- expert_ids: int32 [512, 8], P(('groups', 'expert')), parts along dimension 0, may hold values from 0 to 63, as said below
- slot_ids: int32 [512, 8], P(('groups', 'expert')), parts along dimension 0, may hold values from 0 to 11, as said below
- gate_num: int32 [512, 8], P(('groups', 'expert')), parts along dimension 0, may hold values from 1 to 255
Outputs:
- layer_out: bfloat16 [512, 4096], P(('groups', 'expert'), 'hidden'), parts along dimension 0
There are 2 independent parts, one for each index of `groups`. A program takes and returns all parts, laid end to end along the dimension named above; an argument that names none is the same for every part. Nothing has to cross between parts.
Inputs may be any that keep to these rules, and one draw needn't show every extreme that they name: `expert_ids`: each token names 8 different experts. In every aligned block of 64 tokens (the tokens of one index of the expert axis), a quarter of the experts are named by exactly 12 tokens, a quarter by 8 and the other half by 6; some expert is named by 12 tokens in every block. `slot_ids`: within an aligned block of 64 tokens, the routes that name one expert carry the slots 0 up to their count minus 1, each once.
All inputs are finite; a program needn't handle non-finite values.
Results may differ from a plain program's by a relative error of at most 0.0085.
Values may be sent and summed in bfloat16 or wider, within the bound.
A program may use at most 128 MiB of HBM per device.

v0:
```python
import jax
import jax.numpy as jnp
from jax import lax
from jax.sharding import PartitionSpec as P

D = 4096
SPECIALIST_COUNT = 64
CAP = 12


gate_scale = 1.0 / 1024.0


def route_tables(expert_ids, slot_ids, gate_num):
    slot_index = expert_ids * CAP + slot_ids
    columns = lax.broadcasted_iota(jnp.int32, (1, 1, SPECIALIST_COUNT * CAP), 2)
    matches = slot_index[:, :, None] == columns
    placing = jnp.any(matches, axis=1).astype(jnp.bfloat16)
    scaled = gate_num.astype(jnp.float32) * gate_scale
    weights = jnp.sum(jnp.where(matches, scaled[:, :, None], 0.0), axis=1).astype(jnp.bfloat16)
    return (placing, weights)


def normalize(features, gain, total_squares):
    scale = lax.rsqrt(total_squares / D + 0.5)
    return (
        features.astype(jnp.float32) * scale[:, None] * gain.astype(jnp.float32)[None, :]
    ).astype(jnp.bfloat16)


def place_rows(placing, normed, sources):
    outgoing = lax.dot_general(
        placing, normed, (((0,), (0,)), ((), ())), preferred_element_type=jnp.float32
    )
    return outgoing.astype(jnp.bfloat16).reshape(sources, -1, CAP, normed.shape[1])


def on_device(tokens, norm_gain, gate_proj, up_proj, down_proj, expert_ids, slot_ids, gate_num):
    sources = lax.axis_size("expert")
    placing, weights = route_tables(expert_ids, slot_ids, gate_num)
    local_squares = jnp.sum(jnp.square(tokens.astype(jnp.float32)), axis=1)
    squares = lax.psum(local_squares, "hidden")
    normed = normalize(tokens, norm_gain, squares)
    outgoing = place_rows(placing, normed, sources)
    received = lax.all_to_all(outgoing, "expert", split_axis=0, concat_axis=2, tiled=True)[0]
    block_cols = lax.all_gather(received, "hidden", axis=2, tiled=True)
    gate_more = jnp.einsum(
        "ehd,erd->ehr", gate_proj, block_cols, preferred_element_type=jnp.float32
    )
    up_more = jnp.einsum("ehd,erd->ehr", up_proj, block_cols, preferred_element_type=jnp.float32)
    activated = (jax.nn.silu(gate_more) * up_more).astype(jnp.bfloat16)
    partial_value = jnp.einsum(
        "ehr,ehd->erd", activated, down_proj, preferred_element_type=jnp.float32
    ).astype(jnp.bfloat16)
    returned = lax.all_to_all(
        partial_value[None], "expert", split_axis=2, concat_axis=0, tiled=True
    )
    returned = returned.reshape(-1, returned.shape[-1])
    partial_out = jnp.dot(weights, returned, preferred_element_type=jnp.float32)
    return lax.psum_scatter(partial_out, "hidden", scatter_dimension=1, tiled=True).astype(
        jnp.bfloat16
    )


def solution(mesh):
    placed = (
        P(("groups", "expert"), "hidden"),
        P("hidden"),
        P("expert", "hidden", None),
        P("expert", "hidden", None),
        P("expert", "hidden", None),
        P(("groups", "expert"), None),
        P(("groups", "expert"), None),
        P(("groups", "expert"), None),
    )
    return jax.shard_map(
        on_device,
        mesh=mesh,
        in_specs=placed,
        out_specs=P(("groups", "expert"), "hidden"),
        check_vma=False,
    )
```

profile of v0, /device:TPU:0, one launch (start us, length us, event | category | flops | bytes accessed | tf_op | source)
XLA Modules:
  0.0 358.5 jit_solution(16859934131630568120)
XLA Ops:
  6.5 0.0 all-gather.2.cloned.1.call-start
  6.5 0.7 multiply_add_fusion
  7.2 0.1 copy.24
  7.3 0.5 fusion.1
  7.9 0.7 convert_element_type.32
  8.6 1.0 fusion.10
  9.6 8.4 %psum.7 = f32[64]{0:T(128)S(1)} all-reduce(f32[64]{0:T(128)S(1)} %fusion.10), channel_id=1, replica_groups=mesh['groups'=2,'expert'=4,'hidden'=4] {'hidden'}, use_global_device_ids=true, to_apply=%region_3.4 | all-reduce | flops 64 | bytes 512 | tf_op jit(solution)/shard_map/psum | solution.py:42
  18.0 2.7 convolution_convert_fusion.1
  20.7 2.4 reshape.12
  23.1 0.9 copy.26
  23.9 40.4 %all_to_all.30 = bf16[4,16,12,1024]{3,1,2,0:T(8,128)(2,1)S(1)} all-to-all(bf16[4,16,12,1024]{3,1,2,0:T(8,128)(2,1)S(1)} %copy.26), channel_id=1, replica_groups=mesh['groups'=2,'expert'=4,'hidden'=4] {'expert'}, dimensions={0} | all-to-all | bytes 3145728 | tf_op jit(solution)/shard_map/all_to_all | solution.py:45
  64.4 2.0 copy.27
  66.4 0.0 all-gather.2.cloned.1.call-update
  66.4 45.7 %all-gather.2.cloned.1.call-done = bf16[16,48,4096]{2,1,0:T(8,128)(2,1)} async-done(((bf16[16,48,1024]{2,1,0:T(8,128)(2,1)}), bf16[16,48,4096]{2,1,0:T(8,128)(2,1)}) %all-gather.2.cloned.1.call-update) | async-done | bytes 6291472 | tf_op jit(solution)/shard_map/all_gather | solution.py:46
  112.0 14.1 %convolution_bitcast_fusion.1 = f32[16,192,48]{1,2,0:T(8,128)S(1)} fusion(bf16[16,48,4096]{2,1,0:T(8,128)(2,1)} %all-gather.2.cloned.1.call-done, bf16[16,192,4096]{2,1,0:T(8,128)(2,1)} %param.10), kind=kOutput, calls=%fused_computation.7 | convolution fusion | flops 1207959552 | bytes 32047104 | tf_op jit(solution)/shard_map/ehd,erd->ehr/dot_general | solution.py:47
  126.2 22.9 %fusion = bf16[1,16,48,4096]{3,2,1,0:T(8,128)(2,1)} fusion(bf16[16,192,4096]{2,1,0:T(8,128)(2,1)} %param.12, bf16[16,48,4096]{2,1,0:T(8,128)(2,1)} %all-gather.2.cloned.1.call-done, bf16[16,192,4096]{2,1,0:T(8,128)(2,1)} %param.11, f32[16,192,48]{1,2,0:T(8,128)S(1)} %convolution_bitcast_fusion.1), kind=kOutput, calls=%fused_computation.1 | convolution fusion | flops 2419949568 | bytes 63504384 | tf_op jit(solution)/shard_map/ehr,ehd->erd/dot_general | solution.py:52
  149.1 8.9 %copy.28 = bf16[1,16,48,4096]{3,1,0,2:T(8,128)(2,1)} copy(bf16[1,16,48,4096]{3,2,1,0:T(8,128)(2,1)} %fusion) | data formatting | bytes 12582912 | tf_op jit(solution)/shard_map/broadcast_in_dim | solution.py:56
  158.0 0.0 copy-start
  158.0 5.4 %all-to-all-start.1 = ((bf16[1,16,48,4096]{3,1,0,2:T(8,128)(2,1)}), bf16[1,16,48,4096]{3,1,0,2:T(8,128)(2,1)}, u32[]{:S(2)}, u32[]{:S(2)}) async-start(bf16[1,16,48,4096]{3,1,0,2:T(8,128)(2,1)} %copy.28), calls=%async_computation.1 | async-start | bytes 12582912 | tf_op jit(solution)/shard_map/all_to_all | solution.py:55
  163.5 0.3 reduce-scatter.2.cloned.1.call-start
  163.7 0.0 copy-done
  163.7 0.1 copy.25
  163.8 0.6 select_reduce_fusion
  164.4 137.9 %all-to-all-done.1 = bf16[1,16,48,4096]{3,1,0,2:T(8,128)(2,1)} async-done(((bf16[1,16,48,4096]{3,1,0,2:T(8,128)(2,1)}), bf16[1,16,48,4096]{3,1,0,2:T(8,128)(2,1)}, u32[]{:S(2)}, u32[]{:S(2)}) %all-to-all-start.1) | async-done | bytes 6291488 | tf_op jit(solution)/shard_map/all_to_all | solution.py:55
  302.3 9.8 %copy.29 = bf16[4,1,16,12,4096]{4,3,2,0,1:T(8,128)(2,1)} copy(bf16[4,1,16,12,4096]{4,2,3,0,1:T(8,128)(2,1)} %bitcast.7) | data formatting | bytes 12582912 | tf_op jit(solution)/shard_map/all_to_all | solution.py:55
  312.1 9.9 %reshape.13 = bf16[768,4096]{1,0:T(8,128)(2,1)} reshape(bf16[4,1,16,12,4096]{4,3,2,0,1:T(8,128)(2,1)} %copy.29) | data formatting | bytes 12582912 | tf_op jit(solution)/shard_map/reshape | solution.py:58
  322.0 5.0 %fusion.19 = f32[64,4096]{1,0:T(8,128)} fusion(bf16[64,768]{1,0:T(8,128)(2,1)S(1)} %select_reduce_fusion, bf16[768,4096]{1,0:T(8,128)(2,1)} %reshape.13), kind=kOutput, calls=%fused_computation.29 | convolution fusion | flops 402653184 | bytes 7438336 | tf_op jit(solution)/shard_map/dot_general | solution.py:59
  327.0 0.0 reduce-scatter.2.cloned.1.call-update
  327.0 23.0 %reduce-scatter.2.cloned.1.call-done = f32[64,1024]{1,0:T(8,128)} async-done(((f32[64,4096]{1,0:T(8,128)}), f32[64,1024]{1,0:T(8,128)}) %reduce-scatter.2.cloned.1.call-update) | async-done | bytes 262160 | tf_op jit(solution)/shard_map/reduce_scatter | solution.py:60
  350.0 1.6 convert_element_type.37
  (2 shorter events, 0.0 us)
Async XLA Ops:
  6.5 105.5 %all-gather.2.cloned.1.call-start = ((), (), s32[]{:S(2)}) async-start(), calls=%async_computation.3 | async-start | bytes 7864320 | tf_op jit(solution)/shard_map/all_gather | solution.py:46
  158.0 5.7 %copy-start = (s32[64,8]{0,1:T(8,128)S(1)}, s32[64,8]{0,1:T(8,128)}, u32[]{:S(2)}) copy-start(s32[64,8]{0,1:T(8,128)} %param.15) | copy-start | bytes 6148
  158.0 144.3 %all-to-all-start.1 = ((bf16[1,16,48,4096]{3,1,0,2:T(8,128)(2,1)}), bf16[1,16,48,4096]{3,1,0,2:T(8,128)(2,1)}, u32[]{:S(2)}, u32[]{:S(2)}) async-start(bf16[1,16,48,4096]{3,1,0,2:T(8,128)(2,1)} %copy.28), calls=%async_computation.1 | async-start | bytes 12582912 | tf_op jit(solution)/shard_map/all_to_all | solution.py:55
  163.5 186.6 %reduce-scatter.2.cloned.1.call-start = ((), (), s32[]{:S(2)}) async-start(), calls=%async_computation.4 | async-start | bytes 1310720 | tf_op jit(solution)/shard_map/reduce_scatter | solution.py:60
Sparse Core Ops, SparseCore 0:
  66.5 45.4 all-gather.1
  327.1 22.8 reduce-scatter.1
where the time goes:
time: 359 us; the launch traced here: 358 us
  waiting for transfers between devices  207 us (58%)
  blocking collectives  48.8 us (14%)
  matrix products  44.7 us (12%)
  local copies, waits for them, and re-layouts  34 us (9%)
  between operations  13.5 us (4%)
  starting transfers between devices  5.71 us (2%)
  other arithmetic  5.15 us (1%)
    all_to_all x1, waiting for transfers between devices, on_device(): lax.all_to_all(partial_value[None], 'expert', split_axis=2, concat_axis=0...  138 us
    all_gather x1, waiting for transfers between devices, on_device(): block_cols = lax.all_gather(received, 'hidden', axis=2, tiled=True)  45.7 us
    all_to_all x1, blocking collectives, on_device(): lax.all_to_all(outgoing, 'expert', split_axis=0, concat_axis=2, tiled=True)  40.4 us
    reduce_scatter x1, waiting for transfers between devices, on_device(): lax.psum_scatter(partial_out, 'hidden', scatter_dimension=1, tiled=True)  23 us
    dot_general x1, matrix products, on_device(): jnp.einsum('ehr,ehd->erd', activated, down_proj, preferred_element_type=j...  22.9 us
    dot_general x1, matrix products, on_device(): jnp.einsum('ehd,erd->ehr', gate_proj, block_cols, preferred_element_type=...  14.1 us
    reshape x1, local copies, waits for them, and re-layouts, on_device(): returned = returned.reshape(-1, returned.shape[-1])  9.85 us
    all_to_all x1, local copies, waits for them, and re-layouts, on_device(): lax.all_to_all(partial_value[None], 'expert', split_axis=2, concat_axis=0...  9.84 us
  transfers between devices with their start and end apart: 3, of which 3 were waited for; matrix products, arithmetic and copies ran while one was open for 0% of the time, Pallas kernels for 0%

commit v1 on v0

--- a/solution.py
+++ b/solution.py
@@ -1,6 +1,10 @@
+import functools
+
 import jax
 import jax.numpy as jnp
 from jax import lax
+from jax.experimental import pallas as pl
+from jax.experimental.pallas import tpu as pltpu
 from jax.sharding import PartitionSpec as P
 
 D = 4096
@@ -62,7 +66,308 @@
     )
 
 
+MESH = pl.DeviceIdType.MESH
+PACK = 1024
+
+
+def fused_kernel(
+    dims, tok_ref, gain_ref, route_ref, gate_ref, up_ref, down_ref, out_ref,
+    wbuf, xall, xn, gbuf, rtab, wcol, abuf, pbuf, sibr, r1, r2m, r2p, r3t, r3b, r4, r5m, r5p, tbuf,
+    wsem, dsem, lsem, ssem, rsem,
+):
+    rows, feat, per, units, experts, slots = dims
+    half = rows // 2
+    zn, hn = 4, 4
+    d = feat * hn
+    group = per * units
+    z = lax.axis_index("expert")
+    h = lax.axis_index("hidden")
+    g = lax.axis_index("groups")
+    x, c = h // 2, h % 2
+    zp, zm, z2 = (z + 1) % zn, (z + 3) % zn, (z + 2) % zn
+    hx = (1 - x) * 2 + c
+    hs = x * 2 + (1 - c)
+    hd = (1 - x) * 2 + (1 - c)
+    XP, SIB = (g, z, hx), (g, z, hs)
+    ZP, ZM, Z2 = (g, zp, h), (g, zm, h), (g, z2, h)
+
+    def weight_copies(p):
+        out = []
+        for i in range(per):
+            for j, ref in enumerate((gate_ref, up_ref)):
+                out.append(pltpu.make_async_copy(
+                    ref.at[per * p + i],
+                    wbuf.at[p, pl.ds(j * group + i * units, units), :],
+                    wsem.at[p, per * j + i],
+                ))
+        return out
+
+    def down_copies(s):
+        return [
+            pltpu.make_async_copy(
+                down_ref.at[2 * per * s + i], wbuf.at[s, pl.ds(i * units, units), :], dsem.at[s, i]
+            )
+            for i in range(2 * per)
+        ]
+
+    for p in range(slots):
+        for copy in weight_copies(p):
+            copy.start()
+
+    barrier = pltpu.get_barrier_semaphore()
+    for peer in (XP, SIB, ZP, ZM, Z2):
+        pl.semaphore_signal(barrier, inc=1, device_id=peer, device_id_type=MESH)
+    pl.semaphore_wait(barrier, 5)
+
+    sends = []
+
+    def send(index, src, dst, peer):
+        copy = pltpu.make_async_remote_copy(
+            src_ref=src, dst_ref=dst, send_sem=ssem.at[index], recv_sem=rsem.at[index],
+            device_id=peer, device_id_type=MESH,
+        )
+        copy.start()
+        sends.append(copy)
+
+    def arrived(index, dst):
+        pltpu.make_async_remote_copy(
+            src_ref=dst, dst_ref=dst, send_sem=ssem.at[index], recv_sem=rsem.at[index],
+            device_id=SIB, device_id_type=MESH,
+        ).wait_recv()
+
+    def blk(hh, zz):
+        return xall.at[hh, pl.ds(pl.multiple_of(zz * rows, rows), rows), :]
+
+    def blk_half(hh, zz, which):
+        return xall.at[hh, pl.ds(pl.multiple_of(zz * rows + which * half, half), half), :]
+
+    send(0, tok_ref, blk(h, z), XP)
+    send(1, tok_ref, blk(h, z), ZP)
+    send(2, tok_ref, blk(h, z), ZM)
+    send(3, gain_ref, gbuf.at[h], XP)
+    send(4, route_ref, rtab.at[z], ZP)
+    send(5, route_ref, rtab.at[z], ZM)
+    send(6, route_ref, rtab.at[z], Z2)
+    send(7, gain_ref, gbuf.at[h], SIB)
+    send(8, tok_ref, blk(h, z), SIB)
+    local = [
+        pltpu.make_async_copy(tok_ref, blk(h, z), lsem.at[0]),
+        pltpu.make_async_copy(gain_ref, gbuf.at[h], lsem.at[1]),
+        pltpu.make_async_copy(route_ref, rtab.at[z], lsem.at[2]),
+    ]
+    for copy in local:
+        copy.start()
+    arrived(1, blk(h, zm))
+    send(9, blk_half(h, zm, 0), blk_half(h, zm, 0), ZP)
+    arrived(2, blk(h, zp))
+    send(10, blk_half(h, zp, 1), blk_half(h, zp, 1), ZM)
+    arrived(0, blk(hx, z))
+    send(11, blk(hx, z), blk(hx, z), ZP)
+    send(12, blk(hx, z), blk(hx, z), ZM)
+    send(13, blk(h, zm), blk(h, zm), SIB)
+    send(14, blk(h, zp), blk(h, zp), SIB)
+    send(15, blk(hx, z), blk(hx, z), SIB)
+    arrived(3, gbuf.at[hx])
+    send(16, gbuf.at[hx], gbuf.at[hx], SIB)
+    arrived(9, blk_half(h, z2, 0))
+    arrived(10, blk_half(h, z2, 1))
+    send(17, blk(h, z2), blk(h, z2), XP)
+    send(18, blk(h, z2), blk(h, z2), SIB)
+
+    for copy in local:
+        copy.wait()
+    arrived(4, rtab.at[zm])
+    arrived(5, rtab.at[zp])
+    arrived(6, rtab.at[z2])
+    lanes = wcol.shape[1]
+    named = lax.broadcasted_iota(jnp.int32, (lanes, rows), 0) + z * experts
+    for zb in range(zn):
+        total = jnp.zeros((lanes, rows), jnp.int32)
+        for k in range(rtab.shape[1]):
+            row = rtab[zb, k : k + 1, :]
+            total = total + jnp.where((row >> 10) == named, row & (PACK - 1), 0)
+        wcol[zb * rows : (zb + 1) * rows, :] = (total.astype(jnp.float32) * gate_scale).T
+
+    arrived(11, blk(hx, zm))
+    send(19, blk(hx, zm), blk(hx, zm), SIB)
+    arrived(12, blk(hx, zp))
+    send(20, blk(hx, zp), blk(hx, zp), SIB)
+    arrived(17, blk(hx, z2))
+    send(21, blk(hx, z2), blk(hx, z2), SIB)
+    arrived(7, gbuf.at[hs])
+    arrived(16, gbuf.at[hd])
+    arrived(8, blk(hs, z))
+    arrived(13, blk(hs, zm))
+    arrived(14, blk(hs, zp))
+    arrived(15, blk(hd, z))
+    arrived(18, blk(hs, z2))
+    arrived(19, blk(hd, zm))
+    arrived(20, blk(hd, zp))
+    arrived(21, blk(hd, z2))
+
+    def normal(i, carry):
+        at = pl.ds(pl.multiple_of(i * half, half), half)
+        squares = jnp.zeros((half, 1), jnp.float32)
+        for hh in range(hn):
+            piece = xall[hh, at, :].astype(jnp.float32)
+            squares = squares + jnp.sum(piece * piece, axis=1, keepdims=True)
+        scale = lax.rsqrt(squares / d + 0.5)
+        for hh in range(hn):
+            piece = xall[hh, at, :].astype(jnp.float32)
+            xn[at, hh * feat : (hh + 1) * feat] = (piece * scale * gbuf[hh]).astype(jnp.bfloat16)
+        return carry
+
+    lax.fori_loop(0, 2 * zn, normal, 0)
+
+    def expert_pair(p):
+        for copy in weight_copies(p):
+            copy.wait()
+        both = lax.dot_general(
+            xn[...], wbuf[p], (((1,), (1,)), ((), ())), preferred_element_type=jnp.float32
+        )
+        gate, up = both[:, :group], both[:, group:]
+        table = wcol[...]
+        lane = lax.broadcasted_iota(jnp.int32, table.shape, 1)
+        wide = lax.broadcasted_iota(jnp.int32, gate.shape, 1)
+        weight = jnp.zeros(gate.shape, jnp.float32)
+        for i in range(per):
+            col = jnp.sum(jnp.where(lane == per * p + i, table, 0.0), axis=1, keepdims=True)
+            weight = jnp.where((wide >= i * units) & (wide < (i + 1) * units), col, weight)
+        act = gate / (1.0 + jnp.exp(-gate)) * up
+        act = jnp.where(weight > 0.0, act * weight, 0.0)
+        abuf[:, pl.ds(pl.multiple_of(p * group, 128), group)] = act.astype(jnp.bfloat16)
+
+    def first(p, carry):
+        expert_pair(p)
+        for copy in down_copies(p):
+            copy.start()
+        return carry
+
+    def second(p, carry):
+        expert_pair(p)
+        return carry
+
+    lax.fori_loop(0, slots // 2, first, 0)
+    lax.fori_loop(slots // 2, slots, second, 0)
+    for s in range(slots // 2):
+        for copy in down_copies(s):
+            copy.wait()
+
+    tile = 256
+
+    def down(hh, place):
+        def body(i, carry):
+            cols = pl.ds(pl.multiple_of(hh * feat + i * tile, tile), tile)
+            dense = wbuf[: slots // 2, :, cols].reshape(-1, tile)
+            value = jnp.dot(abuf[...], dense, preferred_element_type=jnp.float32)
+            pbuf[place, :, pl.ds(pl.multiple_of(i * tile, tile), tile)] = value.astype(jnp.bfloat16)
+            return carry
+
+        lax.fori_loop(0, feat // tile, body, 0)
+
+    f32, b16 = jnp.float32, jnp.bfloat16
+
+    def join(place, other):
+        def body(i, carry):
+            at = pl.ds(pl.multiple_of(i * rows, rows), rows)
+            value = pbuf[place, at, :].astype(f32) + sibr[other, at, :].astype(f32)
+            pbuf[place, at, :] = value.astype(b16)
+            return carry
+
+        lax.fori_loop(0, zn, body, 0)
+
+    def at_rows(zz):
+        return pl.ds(pl.multiple_of(zz * rows, rows), rows)
+
+    def at_half(zz, which):
+        return pl.ds(pl.multiple_of(zz * rows + which * half, half), half)
+
+    down(hd, 0)
+    send(22, pbuf.at[0], sibr.at[0], SIB)
+    down(hx, 1)
+    arrived(22, sibr.at[0])
+    join(1, 0)
+    send(23, pbuf.at[1, at_rows(z2), :], r1, XP)
+    send(24, pbuf.at[1, at_rows(zp), :], r2m, ZP)
+    send(25, pbuf.at[1, at_rows(zm), :], r2p, ZM)
+    down(hs, 2)
+    send(26, pbuf.at[2], sibr.at[1], SIB)
+    down(h, 3)
+    arrived(26, sibr.at[1])
+    join(3, 1)
+    arrived(23, r1)
+    tbuf[0] = (pbuf[3, at_rows(z2), :].astype(f32) + r1[...].astype(f32)).astype(b16)
+    send(27, tbuf.at[0, pl.ds(0, half), :], r3t, ZP)
+    send(28, tbuf.at[0, pl.ds(half, half), :], r3b, ZM)
+    send(29, pbuf.at[3, at_half(zp, 1), :], r5m.at[pl.ds(half, half), :], ZP)
+    send(30, pbuf.at[3, at_half(zm, 0), :], r5p.at[pl.ds(0, half), :], ZM)
+    arrived(24, r2m)
+    arrived(25, r2p)
+    tbuf[1] = (pbuf[1, at_rows(z), :].astype(f32) + r2m[...].astype(f32) + r2p[...].astype(f32)).astype(b16)
+    send(31, tbuf.at[1], r4, XP)
+    arrived(27, r3t)
+    tbuf[2, 0:half, :] = (pbuf[3, at_half(zp, 0), :].astype(f32) + r3t[...].astype(f32)).astype(b16)
+    send(32, tbuf.at[2, pl.ds(0, half), :], r5m.at[pl.ds(0, half), :], ZP)
+    arrived(28, r3b)
+    tbuf[2, half:rows, :] = (pbuf[3, at_half(zm, 1), :].astype(f32) + r3b[...].astype(f32)).astype(b16)
+    send(33, tbuf.at[2, pl.ds(half, half), :], r5p.at[pl.ds(half, half), :], ZM)
+    arrived(31, r4)
+    arrived(29, r5m.at[pl.ds(half, half), :])
+    arrived(30, r5p.at[pl.ds(0, half), :])
+    arrived(32, r5m.at[pl.ds(0, half), :])
+    arrived(33, r5p.at[pl.ds(half, half), :])
+    out_ref[...] = (
+        pbuf[3, at_rows(z), :].astype(f32) + r4[...].astype(f32) + r5m[...].astype(f32) + r5p[...].astype(f32)
+    ).astype(b16)
+    for copy in sends:
+        copy.wait_send()
+
+
+def fused_on_device(tokens, norm_gain, gate_proj, up_proj, down_proj, expert_ids, slot_ids, gate_num):
+    rows, feat = tokens.shape
+    experts, units, d = gate_proj.shape
+    zn, per = lax.axis_size("expert"), 2
+    slots = experts // per
+    total = rows * zn
+    packed = (expert_ids * PACK + gate_num).T
+    bf = jnp.bfloat16
+    dims = (rows, feat, per, units, experts, slots)
+    vm = pl.BlockSpec(memory_space=pltpu.VMEM)
+    anywhere = pl.BlockSpec(memory_space=pl.ANY)
+    block = pltpu.VMEM((rows, feat), bf)
+    small = pltpu.VMEM((rows // 2, feat), bf)
+    dma = pltpu.SemaphoreType.DMA
+    return pl.pallas_call(
+        functools.partial(fused_kernel, dims),
+        out_shape=jax.ShapeDtypeStruct((rows, feat), bf),
+        in_specs=[vm, vm, vm, anywhere, anywhere, anywhere],
+        out_specs=vm,
+        scratch_shapes=[
+            pltpu.VMEM((slots, 2 * per * units, d), bf),
+            pltpu.VMEM((d // feat, total, feat), bf),
+            pltpu.VMEM((total, d), bf),
+            pltpu.VMEM((d // feat, 1, feat), jnp.float32),
+            pltpu.VMEM((zn,) + packed.shape, jnp.int32),
+            pltpu.VMEM((total, 128), jnp.float32),
+            pltpu.VMEM((total, experts * units), bf),
+            pltpu.VMEM((4, total, feat), bf),
+            pltpu.VMEM((2, total, feat), bf),
+            block, block, block, small, small, block, block, block,
+            pltpu.VMEM((3, rows, feat), bf),
+            dma((slots, 2 * per)),
+            dma((slots // 2, 2 * per)),
+            dma((3,)),
+            dma((34,)),
+            dma((34,)),
+        ],
+        compiler_params=pltpu.CompilerParams(
+            collective_id=0, has_side_effects=True, vmem_limit_bytes=67043328
+        ),
+    )(tokens, norm_gain.astype(jnp.float32)[None, :], packed, gate_proj, up_proj, down_proj)
+
+
 def solution(mesh):
+    square = mesh.shape["expert"] == 4 and mesh.shape["hidden"] == 4
     placed = (
         P(("groups", "expert"), "hidden"),
         P("hidden"),
@@ -74,7 +379,7 @@
         P(("groups", "expert"), None),
     )
     return jax.shard_map(
-        on_device,
+        fused_on_device if square else on_device,
         mesh=mesh,
         in_specs=placed,
         out_specs=P(("groups", "expert"), "hidden"),

time: 359 us -> 67.2 us (0.19)
  waiting for transfers between devices: 207 us -> 0 us
  Pallas kernels: 0 us -> 62.9 us
  blocking collectives: 48.8 us -> 0 us
  matrix products: 44.7 us -> 0 us
  local copies, waits for them, and re-layouts: 34 us -> 1.57 us
  between operations: 13.5 us -> 0.01 us
  starting transfers between devices: 5.71 us -> 0 us
    all_to_all x1 -> x0, waiting for transfers between devices: 138 us -> none  [on_device(): lax.all_to_all(partial_value[None], 'expert', split_axis=2, concat_axis=0...]
    pallas_call x0 -> x1, Pallas kernels: none -> 62.9 us  [fused_on_device(): pl.pallas_call(functools.partial(fused_kernel, dims), out_shape=jax.Shape...]
    all_gather x1 -> x0, waiting for transfers between devices: 45.7 us -> none  [on_device(): block_cols = lax.all_gather(received, 'hidden', axis=2, tiled=True)]
    dot_general x4 -> x0, matrix products: 44.7 us -> none  [the longest x1 22.9 us: on_device(): jnp.einsum('ehr,ehd->erd', activated, down_proj, preferred_element_type=j...]
    all_to_all x1 -> x0, blocking collectives: 40.4 us -> none  [on_device(): lax.all_to_all(outgoing, 'expert', split_axis=0, concat_axis=2, tiled=True)]
    reduce_scatter x1 -> x0, waiting for transfers between devices: 23 us -> none  [on_device(): lax.psum_scatter(partial_out, 'hidden', scatter_dimension=1, tiled=True)]
    reshape x3 -> x0, local copies, waits for them, and re-layouts: 13.1 us -> none  [the longest x1 9.85 us: on_device(): returned = returned.reshape(-1, returned.shape[-1])]
    all_to_all x1 -> x0, local copies, waits for them, and re-layouts: 9.84 us -> none  [on_device(): lax.all_to_all(partial_value[None], 'expert', split_axis=2, concat_axis=0...]
  transfers between devices with their start and end apart: 3 -> 0, of which waited for: 3 -> 0; matrix products, arithmetic and copies ran while one was open for 0% -> 0% of each run, Pallas kernels for 0% -> 0%
where the time goes in v1:
time: 67.2 us; the launch traced here: 67 us
  Pallas kernels  62.9 us (94%)
  other arithmetic  2.57 us (4%)
  local copies, waits for them, and re-layouts  1.57 us (2%)
    pallas_call x1, Pallas kernels, fused_on_device(): pl.pallas_call(functools.partial(fused_kernel, dims), out_shape=jax.Shape...  62.9 us
    unnamed x1, local copies, waits for them, and re-layouts  1.57 us

profile of v1, /device:TPU:0, one launch (start us, length us, event | category | flops | bytes accessed | tf_op | source)
XLA Modules:
  0.0 67.0 jit_solution(17195241396620768112)
XLA Ops:
  0.0 1.3 %broadcast_in_dim.7 = f32[1024]{0:T(1024)} convert(bf16[1024]{0:T(1024)(128)(2,1)} %param.9) | non-fusion elementwise | flops 1024 | bytes 6144 | tf_op jit(solution)/shard_map/broadcast_in_dim | solution.py:366
  1.3 1.3 %add_bitcast_fusion.route_ref = s32[8,64]{1,0:T(8,128)} fusion(s32[64,8]{0,1:T(8,128)} %param.14, s32[64,8]{0,1:T(8,128)} %param.13), kind=kLoop, calls=%fused_computation | loop fusion | flops 1024 | bytes 6144 | tf_op jit(solution)/shard_map/transpose | solution.py:332
  2.6 62.9 %shard_map.73 = bf16[64,1024]{1,0:T(8,128)(2,1)} custom-call(bf16[64,1024]{1,0:T(8,128)(2,1)} %tok_ref.1, f32[1,1024]{1,0:T(1,128)} %bitcast.3, s32[8,64]{1,0:T(8,128)} %add_bitcast_fusion.route_ref, bf16[16,192,4096]{2,1,0:T(8,128)(2,1)} %gate_ref.1, bf16[16,192,4096]{2,1,0:T(8,128)(2,1)} %up_ref.1, bf16[16,192,4096]{2,1,0:T(8,128)(2,1)} %down_ref.1), custom_call_target="tpu_custom_call" | custom-call | tf_op jit(solution)/shard_map/pallas_call | solution.py:340
  65.4 1.6 %copy.9 = bf16[64,1024]{1,0:T(8,128)(2,1)} copy(bf16[64,1024]{1,0:T(8,128)(2,1)} %shard_map.73) | data formatting | bytes 262144

commit v2 on v0

--- a/solution.py
+++ b/solution.py
@@ -1,6 +1,10 @@
+import functools
+
 import jax
 import jax.numpy as jnp
 from jax import lax
+from jax.experimental import pallas as pl
+from jax.experimental.pallas import tpu as pltpu
 from jax.sharding import PartitionSpec as P
 
 D = 4096
@@ -62,7 +66,362 @@
     )
 
 
+MESH = pl.DeviceIdType.MESH
+
+
+def fused_kernel(
+    dims, tok_ref, gain_ref, ids_ref, num_ref, gate_ref, up_ref, down_ref, out_ref,
+    wbuf, xall, xn, gbuf, rtab, wcol, abuf, pbuf, sibr, rx, ob, qb, ib, tbuf,
+    wsem, dsem, lsem, ssem, rsem,
+):
+    rows, feat, per, units, experts, slots = dims
+    half = rows // 2
+    zn, hn = 4, 4
+    near = 2 * rows
+    d = feat * hn
+    topk = ids_ref.shape[0]
+    group = per * units
+    z = lax.axis_index("expert")
+    h = lax.axis_index("hidden")
+    g = lax.axis_index("groups")
+    x, c = h // 2, h % 2
+    z1, z3 = z + 1 - 2 * (z % 2), 3 - z
+    z2 = (z + 2) % 4
+    is_inner = (z == 1) | (z == 2)
+    is_outer = (z == 0) | (z == 3)
+    inner = (z % 2 + z // 2) % 2
+    hx = (1 - x) * 2 + c
+    hs = x * 2 + (1 - c)
+    hd = (1 - x) * 2 + (1 - c)
+    XP, SIB, NEAR, ACROSS = (g, z, hx), (g, z, hs), (g, z1, h), (g, z3, h)
+    f32, b16 = jnp.float32, jnp.bfloat16
+
+    def weight_copies(p):
+        out = []
+        for i in range(per):
+            for j, ref in enumerate((gate_ref, up_ref)):
+                out.append(pltpu.make_async_copy(
+                    ref.at[per * p + i],
+                    wbuf.at[p, pl.ds(j * group + i * units, units), :],
+                    wsem.at[p, per * j + i],
+                ))
+        return out
+
+    def down_copies(s):
+        return [
+            pltpu.make_async_copy(
+                down_ref.at[2 * per * s + i], wbuf.at[s, pl.ds(i * units, units), :], dsem.at[s, i]
+            )
+            for i in range(2 * per)
+        ]
+
+    barrier = pltpu.get_barrier_semaphore()
+    for peer in (XP, SIB, NEAR):
+        pl.semaphore_signal(barrier, inc=1, device_id=peer, device_id_type=MESH)
+
+    @pl.when(is_inner)
+    def _():
+        pl.semaphore_signal(barrier, inc=1, device_id=ACROSS, device_id_type=MESH)
+
+    pl.semaphore_wait(barrier, 3 + inner)
+
+    numbers, sends = {}, []
+
+    def number(key):
+        return numbers.setdefault(key, len(numbers))
+
+    def make(key, tail, src, dst, peer):
+        return pltpu.make_async_remote_copy(
+            src_ref=src, dst_ref=dst, send_sem=ssem.at[number(key + tail)], recv_sem=rsem.at[number(key)],
+            device_id=peer, device_id_type=MESH,
+        )
+
+    def send(key, src, dst, peer, when=None, tail=()):
+        copy = make(key, tail, src, dst, peer)
+        sends.append((copy, when))
+        if when is None:
+            copy.start()
+        else:
+            pl.when(when)(copy.start)
+
+    def arrived(key, dst, when=None):
+        copy = make(key, (), dst, dst, SIB)
+        if when is None:
+            copy.wait_recv()
+        else:
+            pl.when(when)(copy.wait_recv)
+
+    def blk(hh, pos, which=None):
+        if which is None:
+            return xall.at[hh, pl.ds(pl.multiple_of(pos * rows, rows), rows), :]
+        return xall.at[hh, pl.ds(pl.multiple_of(pos * rows + which * half, half), half), :]
+
+    def tok(which):
+        return tok_ref.at[pl.ds(which * half, half), :]
+
+    for w in range(2):
+        send(("z", 1, w), tok(w), blk(h, 1, w), NEAR)
+        send(("z", "mid", w), tok(w), blk(h, 3, w), ACROSS, is_inner, ("own",))
+        send(("x", 0, w), tok(w), blk(h, 0, w), XP)
+    for name, ref, at in (("i", ids_ref, 0), ("n", num_ref, topk)):
+        send((name, 1), ref, rtab.at[1, pl.ds(at, topk), :], NEAR)
+        send((name, "mid"), ref, rtab.at[3, pl.ds(at, topk), :], ACROSS, is_inner, ("own",))
+    send(("gx",), gain_ref, gbuf.at[h], XP)
+    send(("gs",), gain_ref, gbuf.at[h], SIB)
+    send(("s", 0), tok_ref, blk(h, 0), SIB)
+    local = [
+        pltpu.make_async_copy(tok_ref, blk(h, 0), lsem.at[0]),
+        pltpu.make_async_copy(gain_ref, gbuf.at[h], lsem.at[1]),
+        pltpu.make_async_copy(ids_ref, rtab.at[0, pl.ds(0, topk), :], lsem.at[2]),
+        pltpu.make_async_copy(num_ref, rtab.at[0, pl.ds(topk, topk), :], lsem.at[3]),
+    ]
+    for copy in local:
+        copy.start()
+
+    for p in range(slots):
+        for copy in weight_copies(p):
+            copy.start()
+
+    def route(pos, at):
+        return rtab.at[pos, pl.ds(at, topk), :]
+
+    place = {0: 0, 1: 1, "mid": 2 + inner, "last": 3 - inner}
+
+    def relay(name, target, there, peer):
+        pos = place[name]
+        for w in range(2):
+            arrived(("z", name, w), blk(h, pos, w))
+            send(("z", target, w), blk(h, pos, w), blk(h, there, w), peer, is_inner, ("on", name))
+            send(("x", name, w), blk(h, pos, w), blk(h, pos, w), XP)
+        for kind, at in (("i", 0), ("n", topk)):
+            arrived((kind, name), route(pos, at))
+            send((kind, target), route(pos, at), route(there, at), peer, is_inner, ("on", name))
+        send(("s", name), blk(h, pos), blk(h, pos), SIB)
+
+    def pass_over(name):
+        pos = place[name]
+        for w in range(2):
+            arrived(("x", name, w), blk(hx, pos, w))
+        send(("t", name), blk(hx, pos), blk(hx, pos), SIB)
+
+    def from_sibling(name):
+        arrived(("s", name), blk(hs, place[name]))
+        arrived(("t", name), blk(hd, place[name]))
+
+    lanes = wcol.shape[1]
+    named = lax.broadcasted_iota(jnp.int32, (lanes, rows), 0) + z * experts
+
+    def weigh(pos):
+        total = jnp.zeros((lanes, rows), jnp.int32)
+        for k in range(topk):
+            total = total + jnp.where(
+                rtab[pos, k : k + 1, :] == named, rtab[pos, topk + k : topk + k + 1, :], 0
+            )
+        wcol[pos * rows : (pos + 1) * rows, :] = (total.astype(f32) * gate_scale).T
+
+    def normal(start):
+        def body(i, carry):
+            at = pl.ds(pl.multiple_of(i * half + start, half), half)
+            squares = jnp.zeros((half, 1), f32)
+            for hh in range(hn):
+                piece = xall[hh, at, :].astype(f32)
+                squares = squares + jnp.sum(piece * piece, axis=1, keepdims=True)
+            scale = lax.rsqrt(squares / d + 0.5)
+            for hh in range(hn):
+                piece = xall[hh, at, :].astype(f32)
+                gain = gbuf[hh].astype(f32)
+                xn[at, hh * feat : (hh + 1) * feat] = (piece * scale * gain).astype(b16)
+            return carry
+
+        lax.fori_loop(0, near // half, body, 0)
+
+    def expert_pair(p):
+        both = lax.dot_general(
+            xn[...], wbuf[p], (((1,), (1,)), ((), ())), preferred_element_type=f32
+        )
+        gate, up = both[:, :group], both[:, group:]
+        table = wcol[...]
+        lane = lax.broadcasted_iota(jnp.int32, table.shape, 1)
+        wide = lax.broadcasted_iota(jnp.int32, gate.shape, 1)
+        weight = jnp.zeros(gate.shape, f32)
+        for i in range(per):
+            col = jnp.sum(jnp.where(lane == per * p + i, table, 0.0), axis=1, keepdims=True)
+            weight = jnp.where((wide >= i * units) & (wide < (i + 1) * units), col, weight)
+        act = gate / (1.0 + jnp.exp(-gate)) * up
+        act = jnp.where(weight > 0.0, act * weight, 0.0)
+        abuf[:, pl.ds(pl.multiple_of(p * group, 128), group)] = act.astype(b16)
+
+    relay(1, "last", 2, ACROSS)
+    relay("mid", "mid", 2, NEAR)
+    pass_over(0)
+    arrived(("gx",), gbuf.at[hx])
+    send(("gt",), gbuf.at[hx], gbuf.at[hx], SIB)
+    for copy in local:
+        copy.wait()
+    relay("last", "last", 3, NEAR)
+    pass_over(1)
+    pass_over("mid")
+    for pos in range(zn):
+        weigh(pos)
+    arrived(("gs",), gbuf.at[hs])
+    arrived(("gt",), gbuf.at[hd])
+    from_sibling(0)
+    from_sibling(1)
+    normal(0)
+    pass_over("last")
+    from_sibling("mid")
+    from_sibling("last")
+    normal(near)
+
+    def first(p, carry):
+        for copy in weight_copies(p):
+            copy.wait()
+        expert_pair(p)
+        for copy in down_copies(p):
+            copy.start()
+        return carry
+
+    def second(p, carry):
+        for copy in weight_copies(p):
+            copy.wait()
+        expert_pair(p)
+        return carry
+
+    lax.fori_loop(0, slots // 2, first, 0)
+    lax.fori_loop(slots // 2, slots, second, 0)
+    for s in range(slots // 2):
+        for copy in down_copies(s):
+            copy.wait()
+
+    tile = 256
+
+    def down(hh, place):
+        def body(i, carry):
+            cols = pl.ds(pl.multiple_of(hh * feat + i * tile, tile), tile)
+            dense = wbuf[: slots // 2, :, cols].reshape(-1, tile)
+            value = jnp.dot(abuf[...], dense, preferred_element_type=f32)
+            pbuf[place, :, pl.ds(pl.multiple_of(i * tile, tile), tile)] = value.astype(b16)
+            return carry
+
+        lax.fori_loop(0, feat // tile, body, 0)
+
+    def part(pos, w):
+        return pl.ds(pl.multiple_of(pos * rows + w * half, half), half)
+
+    order = [3 - inner, 2 + inner, 1, 0]
+    down(hd, 0)
+    send(("c", 0), pbuf.at[0], sibr.at[0], SIB)
+    down(hx, 1)
+    arrived(("c", 0), sibr.at[0])
+    for n, pos in enumerate(order):
+        for w in range(2):
+            at = part(pos, w)
+            pbuf[1, at, :] = (pbuf[1, at, :].astype(f32) + sibr[0, at, :].astype(f32)).astype(b16)
+            send(("o", n, w), pbuf.at[1, at, :], rx.at[at, :], XP)
+    down(hs, 2)
+    send(("c", 1), pbuf.at[2], sibr.at[1], SIB)
+    down(h, 3)
+    arrived(("c", 1), sibr.at[1])
+
+    def wide_at(w):
+        return pl.ds(w * half, half)
+
+    for n, pos in enumerate(order):
+        for w in range(2):
+            at = part(pos, w)
+            arrived(("o", n, w), rx.at[at, :])
+            value = pbuf[3, at, :].astype(f32) + sibr[1, at, :].astype(f32) + rx[at, :].astype(f32)
+            pbuf[3, at, :] = value.astype(b16)
+            if n < 3:
+                send(("e", n, w), pbuf.at[3, at, :], ob.at[n, wide_at(w), :], NEAR, is_outer)
+            if n < 2:
+                arrived(("e", n, w), ob.at[n, wide_at(w), :], is_inner)
+
+                @pl.when(is_inner)
+                def _(n=n, w=w, at=at):
+                    tbuf[n, wide_at(w), :] = (
+                        pbuf[3, at, :].astype(f32) + ob[n, wide_at(w), :].astype(f32)
+                    ).astype(b16)
+
+                send(("q", n, w), tbuf.at[n, wide_at(w), :], qb.at[n, wide_at(w), :], ACROSS, is_inner)
+    for w in range(2):
+        arrived(("q", 0, w), qb.at[0, wide_at(w), :], is_inner)
+
+        @pl.when(is_inner)
+        def _(w=w):
+            tbuf[2, wide_at(w), :] = (
+                pbuf[3, part(1, w), :].astype(f32) + qb[0, wide_at(w), :].astype(f32)
+            ).astype(b16)
+
+        send(("b", w), tbuf.at[2, wide_at(w), :], ib.at[wide_at(w), :], NEAR, is_inner)
+    for w in range(2):
+        at = part(0, w)
+        arrived(("e", 2, w), ob.at[2, wide_at(w), :], is_inner)
+        arrived(("q", 1, w), qb.at[1, wide_at(w), :], is_inner)
+        arrived(("b", w), ib.at[wide_at(w), :], is_outer)
+
+        @pl.when(is_inner)
+        def _(w=w, at=at):
+            out_ref[wide_at(w), :] = (
+                pbuf[3, at, :].astype(f32) + ob[2, wide_at(w), :].astype(f32) + qb[1, wide_at(w), :].astype(f32)
+            ).astype(b16)
+
+        @pl.when(is_outer)
+        def _(w=w, at=at):
+            out_ref[wide_at(w), :] = (pbuf[3, at, :].astype(f32) + ib[wide_at(w), :].astype(f32)).astype(b16)
+
+    for copy, when in sends:
+        if when is None:
+            copy.wait_send()
+        else:
+            pl.when(when)(copy.wait_send)
+
+
+def fused_on_device(tokens, norm_gain, gate_proj, up_proj, down_proj, expert_ids, slot_ids, gate_num):
+    rows, feat = tokens.shape
+    experts, units, d = gate_proj.shape
+    zn, per = lax.axis_size("expert"), 2
+    slots = experts // per
+    total = rows * zn
+    bf = jnp.bfloat16
+    dims = (rows, feat, per, units, experts, slots)
+    vm = pl.BlockSpec(memory_space=pltpu.VMEM)
+    anywhere = pl.BlockSpec(memory_space=pl.ANY)
+    dma = pltpu.SemaphoreType.DMA
+    return pl.pallas_call(
+        functools.partial(fused_kernel, dims),
+        out_shape=jax.ShapeDtypeStruct((rows, feat), bf),
+        in_specs=[vm, vm, vm, vm, anywhere, anywhere, anywhere],
+        out_specs=vm,
+        scratch_shapes=[
+            pltpu.VMEM((slots, 2 * per * units, d), bf),
+            pltpu.VMEM((d // feat, total, feat), bf),
+            pltpu.VMEM((total, d), bf),
+            pltpu.VMEM((d // feat, 1, feat), norm_gain.dtype),
+            pltpu.VMEM((zn, 2 * expert_ids.shape[1], rows), jnp.int32),
+            pltpu.VMEM((total, 128), jnp.float32),
+            pltpu.VMEM((total, experts * units), bf),
+            pltpu.VMEM((4, total, feat), bf),
+            pltpu.VMEM((2, total, feat), bf),
+            pltpu.VMEM((total, feat), bf),
+            pltpu.VMEM((3, rows, feat), bf),
+            pltpu.VMEM((2, rows, feat), bf),
+            pltpu.VMEM((rows, feat), bf),
+            pltpu.VMEM((3, rows, feat), bf),
+            dma((slots, 2 * per)),
+            dma((slots // 2, 2 * per)),
+            dma((4,)),
+            dma((96,)),
+            dma((96,)),
+        ],
+        compiler_params=pltpu.CompilerParams(
+            collective_id=0, has_side_effects=True, vmem_limit_bytes=67043328
+        ),
+    )(tokens, norm_gain[None, :], expert_ids.T, gate_num.T, gate_proj, up_proj, down_proj)
+
+
 def solution(mesh):
+    square = mesh.shape["expert"] == 4 and mesh.shape["hidden"] == 4
     placed = (
         P(("groups", "expert"), "hidden"),
         P("hidden"),
@@ -74,7 +433,7 @@
         P(("groups", "expert"), None),
     )
     return jax.shard_map(
-        on_device,
+        fused_on_device if square else on_device,
         mesh=mesh,
         in_specs=placed,
         out_specs=P(("groups", "expert"), "hidden"),

time: 359 us -> 64.9 us (0.18)
  waiting for transfers between devices: 207 us -> 0 us
  Pallas kernels: 0 us -> 61.9 us
  blocking collectives: 48.8 us -> 0 us
  matrix products: 44.7 us -> 0 us
  local copies, waits for them, and re-layouts: 34 us -> 2.85 us
  between operations: 13.5 us -> 0.01 us
  starting transfers between devices: 5.71 us -> 0 us
  other arithmetic: 5.15 us -> 0 us
    all_to_all x1 -> x0, waiting for transfers between devices: 138 us -> none  [on_device(): lax.all_to_all(partial_value[None], 'expert', split_axis=2, concat_axis=0...]
    pallas_call x0 -> x1, Pallas kernels: none -> 61.9 us  [fused_on_device(): pl.pallas_call(functools.partial(fused_kernel, dims), out_shape=jax.Shape...]
    all_gather x1 -> x0, waiting for transfers between devices: 45.7 us -> none  [on_device(): block_cols = lax.all_gather(received, 'hidden', axis=2, tiled=True)]
    dot_general x4 -> x0, matrix products: 44.7 us -> none  [the longest x1 22.9 us: on_device(): jnp.einsum('ehr,ehd->erd', activated, down_proj, preferred_element_type=j...]
    all_to_all x1 -> x0, blocking collectives: 40.4 us -> none  [on_device(): lax.all_to_all(outgoing, 'expert', split_axis=0, concat_axis=2, tiled=True)]
    reduce_scatter x1 -> x0, waiting for transfers between devices: 23 us -> none  [on_device(): lax.psum_scatter(partial_out, 'hidden', scatter_dimension=1, tiled=True)]
    reshape x3 -> x0, local copies, waits for them, and re-layouts: 13.1 us -> none  [the longest x1 9.85 us: on_device(): returned = returned.reshape(-1, returned.shape[-1])]
    all_to_all x1 -> x0, local copies, waits for them, and re-layouts: 9.84 us -> none  [on_device(): lax.all_to_all(partial_value[None], 'expert', split_axis=2, concat_axis=0...]
  transfers between devices with their start and end apart: 3 -> 0, of which waited for: 3 -> 0; matrix products, arithmetic and copies ran while one was open for 0% -> 0% of each run, Pallas kernels for 0% -> 0%
where the time goes in v2:
time: 64.9 us; the launch traced here: 64.8 us
  Pallas kernels  61.9 us (95%)
  local copies, waits for them, and re-layouts  2.85 us (4%)
    pallas_call x1, Pallas kernels, fused_on_device(): pl.pallas_call(functools.partial(fused_kernel, dims), out_shape=jax.Shape...  61.9 us
    unnamed x1, local copies, waits for them, and re-layouts  1.57 us

profile of v2, /device:TPU:0, one launch (start us, length us, event | category | flops | bytes accessed | tf_op | source)
XLA Modules:
  0.0 64.8 jit_solution(7756414931247277528)
XLA Ops:
  0.0 1.3 %broadcast_in_dim.3.gain_ref = bf16[1,1024]{1,0:T(2,128)(2,1)} reshape(bf16[1024]{0:T(1024)(128)(2,1)} %param.9) | data formatting | bytes 4096 | tf_op jit(solution)/shard_map/broadcast_in_dim | solution.py:420
  1.3 61.9 %shard_map.73 = bf16[64,1024]{1,0:T(8,128)(2,1)} custom-call(bf16[64,1024]{1,0:T(8,128)(2,1)} %tok_ref.1, bf16[1,1024]{1,0:T(2,128)(2,1)} %broadcast_in_dim.3.gain_ref, s32[8,64]{1,0:T(8,128)} %bitcast.2, s32[8,64]{1,0:T(8,128)} %bitcast.3, bf16[16,192,4096]{2,1,0:T(8,128)(2,1)} %gate_ref.1, bf16[16,192,4096]{2,1,0:T(8,128)(2,1)} %up_ref.1, ...), custom_call_target="tpu_custom_call" | custom-call | tf_op jit(solution)/shard_map/pallas_call | solution.py:391
  63.2 1.6 %copy.9 = bf16[64,1024]{1,0:T(8,128)(2,1)} copy(bf16[64,1024]{1,0:T(8,128)(2,1)} %shard_map.73) | data formatting | bytes 262144
